TPU v7x, 32 devices: a whole 2x2x4 slice. The times are simulated.
32 devices in a mesh: node: 32 (over z, y, x, core).
Axes of the slice: x: 2, y: 2, z: 4, core: 2. Of those that a mesh axis runs over, the one named last changes fastest.
Arguments:
- labels: bfloat16 [131072, 512], P('node'), may hold values from -6 to 6
- seed_mask: int32 [131072], P('node'), may hold values 0 or 1
- band_w: bfloat16 [1024, 3, 128, 128], P('node'), may hold values from 0.0009994507 to 1
- far_block: int32 [32, 32, 2], P('node'), may hold values from 0 to 511
- far_tile: int32 [32, 32, 2], P('node'), may hold values from 0 to 31
- far_count: int32 [32, 32], P('node'), may hold values from 0 to 2, as said below
- far_w: bfloat16 [32, 32, 2, 8, 128], P('node'), may hold values from 0.049804688 to 2
Outputs:
- final_labels: bfloat16 [131072, 512], P('node')
- residual: float32 [2, 1024], P(None, 'node')
Inputs may be any that keep to these rules, and one draw needn't show every extreme that they name: `far_count`: in every draw at least one destination shard has all 2 slots live from every source shard; other counts vary from pair to pair.
All inputs are finite; a program needn't handle non-finite values. No bound on the sum of `seed_mask` on one device may be relied on, other than what follows from the above.
Results may differ from a plain program's by a relative error of at most 0.0027.
Values may be sent and summed in bfloat16 or wider, within the bound.
A program may use at most 128 MiB of HBM per device.

v0:
```python
import jax
import jax.numpy as jnp
from jax import lax
from jax.sharding import PartitionSpec as P

ITERS = 2


def with_halo(block, sides, width):
    for axis, dim in sides:
        count = lax.axis_size(axis)
        forward = [(i, i + 1) for i in range(count - 1)]
        forward.append((count - 1, 0))
        backward = [(target, source) for source, target in forward]
        low = lax.ppermute(
            lax.slice_in_dim(block, block.shape[dim] - width, None, axis=dim), axis, forward
        )
        high = lax.ppermute(lax.slice_in_dim(block, 0, width, axis=dim), axis, backward)
        block = jnp.concatenate([low, block, high], axis=dim)
    return block


def fetch_blocks(current, requests, block_rows, classes):
    blocks = current.reshape(-1, block_rows, classes)[requests]
    return lax.all_to_all(blocks, "node", split_axis=0, concat_axis=0, tiled=True)


def cycle_tiles(current, tile_count, tile_rows, classes):
    tiles = current.reshape(tile_count, tile_rows, classes)
    return with_halo(tiles, (("node", 0),), 1)


def body(labels, seed_mask, band_w, far_block, far_tile, far_count, far_w):
    node_rows, classes = labels.shape
    tile_count = band_w.shape[0]
    tile_rows = band_w.shape[2]
    peer_count = far_w.shape[1]
    slot_count = far_w.shape[2]
    block_rows = far_w.shape[3]
    requests = lax.all_to_all(far_block, "node", split_axis=1, concat_axis=0, tiled=True).reshape(
        peer_count, slot_count
    )
    live_slots = jnp.arange(slot_count)[None, :] < far_count[0][:, None]
    weights = jnp.where(live_slots[:, :, None, None], far_w[0], jnp.zeros((), jnp.bfloat16))
    flat_tiles = far_tile[0].reshape(-1)
    weight_sums = jnp.sum(weights, axis=2, dtype=jnp.float32).reshape(-1, tile_rows)
    degree_far = jnp.zeros((tile_count, tile_rows), jnp.float32).at[flat_tiles].add(weight_sums)
    degree = jnp.sum(band_w, axis=(1, 3), dtype=jnp.float32) + degree_far
    slot_weights = weights.reshape(peer_count * slot_count, block_rows, tile_rows)
    onehot = jnp.arange(tile_count)[:, None] == flat_tiles[None, :]
    placed = jnp.where(onehot[:, :, None, None], slot_weights[None], jnp.zeros((), jnp.bfloat16))
    placed = placed.reshape(tile_count, peer_count * slot_count * block_rows, tile_rows)
    seeded = (seed_mask == 1).reshape(tile_count, tile_rows, 1)
    clamped = labels.astype(jnp.float32).reshape(tile_count, tile_rows, classes)
    current = labels
    residuals = []
    for sweep in range(ITERS):
        padded = cycle_tiles(current, tile_count, tile_rows, classes)
        received = fetch_blocks(current, requests, block_rows, classes)
        band_sum = jnp.zeros((tile_count, tile_rows, classes), jnp.float32)
        for offset in (-1, 0, 1):
            source = padded[1 + offset : 1 + offset + tile_count]
            band_sum = band_sum + jnp.einsum(
                "itr,irc->itc", band_w[:, offset + 1], source, preferred_element_type=jnp.float32
            )
        far_sum = jnp.einsum(
            "tqr,qc->trc", placed, received.reshape(-1, classes), preferred_element_type=jnp.float32
        )
        averaged = (band_sum + far_sum) / degree[:, :, None]
        row_scale = jnp.sqrt(jnp.mean(averaged * averaged, axis=2, keepdims=True))
        scaled = averaged / jnp.maximum(row_scale, 0.05)
        fresh = jnp.where(seeded, clamped, scaled).astype(jnp.bfloat16)
        previous = current.astype(jnp.float32).reshape(tile_count, tile_rows, classes)
        residuals.append(jnp.sum(jnp.abs(fresh.astype(jnp.float32) - previous), axis=(1, 2)))
        current = fresh.reshape(node_rows, classes)
    return (current, jnp.stack(residuals))


def solution(mesh):
    placed = (
        P("node", None),
        P("node"),
        P("node", None, None, None),
        P("node", None, None),
        P("node", None, None),
        P("node", None),
        P("node", None, None, None, None),
    )
    return jax.shard_map(
        body,
        mesh=mesh,
        in_specs=placed,
        out_specs=(P("node", None), P(None, "node")),
        check_vma=False,
    )
```

profile of v0, /device:TPU:0, one launch (start us, length us, event | category | flops | bytes accessed | tf_op | source)
XLA Modules:
  0.0 134.0 jit_solution(6983224722722546354)
XLA Ops:
  0.6 0.0 copy-start.6
  0.6 0.0 copy-start.8
  0.7 1.5 %copy.30 = s32[1,32,2]{2,0,1:T(1,128)} copy(s32[1,32,2]{1,2,0:T(2,128)} %param.10) | data formatting | bytes 512 | tf_op args[3]
  2.2 7.5 %all-to-all-start = ((s32[1,32,2]{2,0,1:T(1,128)}), s32[1,32,2]{2,0,1:T(1,128)}, u32[]{:S(2)}, u32[]{:S(2)}) async-start(s32[1,32,2]{2,0,1:T(1,128)} %copy.30), calls=%async_computation | async-start | bytes 32768 | tf_op jit(solution)/shard_map/all_to_all | solution.py:40
  9.6 1.7 %slice_bitcast_fusion = (bf16[1,128,512]{2,1,0:T(8,128)(2,1)}, bf16[1,128,512]{2,1,0:T(8,128)(2,1)}) fusion(bf16[4096,512]{1,0:T(8,128)(2,1)} %param.7), kind=kLoop, calls=%fused_computation.59 | loop fusion | bytes 524288 | tf_op jit(solution)/shard_map/slice | solution.py:18
  11.4 5.1 %collective-permute-start.1 = (bf16[1,128,512]{2,1,0:T(8,128)(2,1)}, bf16[1,128,512]{2,1,0:T(8,128)(2,1)}, u32[]{:S(2)}, u32[]{:S(2)}) collective-permute-start(bf16[1,128,512]{2,1,0:T(8,128)(2,1)} %get-tuple-element.6), channel_id=1, source_target_pairs={{1,0},{2,1},{3,2},{4,3},{5,4},{6,5},{7,6},{8,7},{9,8},{10,9},{11,1... | collective-permute-start | bytes 393224 | tf_op jit(solution)/shard_map/ppermute | solution.py:18
  16.5 0.0 collective-permute-start
  16.5 0.8 copy.27
  17.2 0.1 reshape_squeeze.3
  17.3 0.1 eq.28
  17.5 0.7 iota_compare_fusion.1
  18.2 0.1 lt.51
  18.3 0.1 broadcast_in_dim.74
  18.4 0.1 broadcast_in_dim.75
  18.5 0.5 fusion.39
  19.0 0.1 iota_compare_fusion
  19.1 2.5 %convert_reduce_fusion = f32[32,128]{1,0:T(8,128)S(1)} fusion(bf16[32,3,128,128]{3,2,1,0:T(8,128)(2,1)} %param.9), kind=kLoop, calls=%fused_computation.19 | loop fusion | flops 3141632 | bytes 3162112 | tf_op jit(solution)/shard_map/reduce_sum | solution.py:48
  21.6 1.0 bitcast_select_fusion.1
  22.7 0.0 copy-done.8
  22.7 0.8 convert_reduce_fusion.1
  23.5 0.1 copy.28
  23.6 0.0 copy-start.9
  23.6 0.1 copy.29
  23.7 1.1 scatter_fusion
  24.9 0.0 all-to-all-done
  24.9 0.8 copy.31
  25.7 0.1 copy.32
  25.8 0.1 reshape.183
  25.9 3.6 %gather_fusion = bf16[64,8,512]{2,1,0:T(8,128)(2,1)} fusion(bf16[512,8,512]{2,1,0:T(8,128)(2,1)} %bitcast.77, s32[1024]{0:T(1024)S(1)} %pad_clamp_fusion), kind=kCustom, calls=%fused_computation | custom fusion | bytes 1048832 | tf_op jit(solution)/shard_map/gather | solution.py:24
  29.5 5.8 %all-to-all-start.1 = ((bf16[32,2,8,512]{3,2,1,0:T(8,128)(2,1)}), bf16[32,2,8,512]{3,2,1,0:T(8,128)(2,1)}, u32[]{:S(2)}, u32[]{:S(2)}) async-start(bf16[32,2,8,512]{3,2,1,0:T(8,128)(2,1)} %bitcast.85), calls=%async_computation.1 | async-start | bytes 1048576 | tf_op jit(solution)/shard_map/all_to_all | solution.py:25
  35.3 0.0 copy-done.6
  35.3 0.0 copy-start.11
  35.4 0.0 copy-start
  35.4 6.8 %fusion.29 = f32[32,128,512]{2,1,0:T(8,128)} fusion(bf16[32,128,512]{2,1,0:T(8,128)(2,1)} %bitcast.78, bf16[32,3,128,128]{3,2,1,0:T(8,128)(2,1)S(1)} %copy-done.6), kind=kOutput, calls=%fused_computation.46 | convolution fusion | flops 536870912 | bytes 13631488 | tf_op jit(solution)/shard_map/itr,irc->itc/dot_general | solution.py:63
  42.2 0.0 copy-done.11
  42.2 0.0 collective-permute-done
  42.2 0.0 copy-done
  42.2 5.4 %fusion.17 = f32[32,512,128]{1,2,0:T(8,128)} fusion(bf16[32,128,512]{2,1,0:T(8,128)(2,1)S(1)} %bitcast.79, bf16[1,128,512]{2,1,0:T(8,128)(2,1)} %collective-permute-done, bf16[32,3,128,128]{3,2,1,0:T(8,128)(2,1)S(1)} %copy-done.6), kind=kOutput, calls=%fused_computation.34 | convolution fusion | flops 545259520 | bytes 13762560 | tf_op jit(solution)/shard_map/itr,irc->itc/dot_general | solution.py:63
  47.6 3.3 %all-to-all-done.1 = bf16[32,2,8,512]{3,2,1,0:T(8,128)(2,1)} async-done(((bf16[32,2,8,512]{3,2,1,0:T(8,128)(2,1)}), bf16[32,2,8,512]{3,2,1,0:T(8,128)(2,1)}, u32[]{:S(2)}, u32[]{:S(2)}) %all-to-all-start.1) | async-done | bytes 524320 | tf_op jit(solution)/shard_map/all_to_all | solution.py:25
  50.9 0.0 copy-done.9
  50.9 6.8 %fusion.9 = f32[32,128,512]{2,1,0:T(8,128)} fusion(bf16[512,512,1]{1,0,2:T(8,128)(2,1)} %bitcast.16, pred[32,512]{1,0:T(8,128)(4,1)S(1)} %copy.28, bf16[512,128]{0,1:T(8,128)(2,1)S(1)} %copy.29), kind=kOutput, calls=%fused_computation.22 | convolution fusion | flops 2149580800 | bytes 9060352 | tf_op jit(solution)/shard_map/tqr,qc->trc/dot_general | solution.py:66
  57.7 0.0 collective-permute-done.1
  57.7 0.0 copy-done.1
  57.7 13.6 %multiply_reduce_fusion.1 = (f32[32,128]{1,0:T(8,128)S(1)}, f32[32,128,512]{2,1,0:T(8,128)}) fusion(f32[32,128]{1,0:T(8,128)S(1)} %scatter_fusion, f32[32,128,512]{2,1,0:T(8,128)} %fusion.9, bf16[1,128,512]{2,1,0:T(8,128)(2,1)} %collective-permute-done.1, bf16[32,128,512]{2,1,0:T(8,128)(2,1)S(1)} %bitcast.80, bf16[32,3,128,128]{3,2,1,0:T(8,128)(2,1)S(1)} %copy-done.6, ...), kind=kOutput, calls=%fused_computation.18 | convolution fusion | flops 557838336 | bytes 38961152 | tf_op jit(solution)/shard_map/itr,irc->itc/dot_general | solution.py:63
  71.3 5.0 %fusion.2 = bf16[32,128,512]{2,1,0:T(8,128)(2,1)S(1)} fusion(f32[32,128,512]{2,1,0:T(8,128)} %get-tuple-element.9, f32[32,128]{1,0:T(8,128)S(1)} %maximum_multiply_fusion.1, pred[32,128]{1,0:T(8,128)(4,1)S(1)} %compare_bitcast_fusion, bf16[4096,512]{1,0:T(8,128)(2,1)S(1)} %copy-done.1), kind=kLoop, calls=%fused_computation.9 | loop fusion | flops 8388608 | bytes 16797696 | tf_op jit(solution)/shard_map/convert_element_type | solution.py:72
  76.3 0.0 copy-start.3
  76.3 2.0 %copy-done.3 = bf16[32,128,512]{2,1,0:T(8,128)(2,1)} copy-done((bf16[32,128,512]{2,1,0:T(8,128)(2,1)}, bf16[32,128,512]{2,1,0:T(8,128)(2,1)S(1)}, u32[]{:S(2)}) %copy-start.3) | copy-done | bytes 4194328
  78.3 0.7 fusion.46
  79.0 0.0 collective-permute-start.2
  79.0 3.6 %gather_fusion.1 = bf16[64,8,512]{2,1,0:T(8,128)(2,1)} fusion(bf16[512,8,512]{2,1,0:T(8,128)(2,1)} %bitcast.82, s32[1024]{0:T(1024)S(1)} %pad_clamp_fusion), kind=kCustom, calls=%fused_computation.1 | custom fusion | bytes 1048832 | tf_op jit(solution)/shard_map/gather | solution.py:24
  82.6 5.8 %all-to-all-start.2 = ((bf16[32,2,8,512]{3,2,1,0:T(8,128)(2,1)}), bf16[32,2,8,512]{3,2,1,0:T(8,128)(2,1)}, u32[]{:S(2)}, u32[]{:S(2)}) async-start(bf16[32,2,8,512]{3,2,1,0:T(8,128)(2,1)} %bitcast.84), calls=%async_computation.2 | async-start | bytes 1048576 | tf_op jit(solution)/shard_map/all_to_all | solution.py:25
  88.4 0.0 copy-start.4
  88.4 6.8 %fusion.27 = f32[32,512,128]{1,2,0:T(8,128)} fusion(bf16[32,128,512]{2,1,0:T(8,128)(2,1)} %copy-done.3, bf16[32,3,128,128]{3,2,1,0:T(8,128)(2,1)S(1)} %copy-done.6), kind=kOutput, calls=%fused_computation.44 | convolution fusion | flops 536870912 | bytes 13631488 | tf_op jit(solution)/shard_map/itr,irc->itc/dot_general | solution.py:63
  95.2 5.1 %collective-permute-start.3 = (bf16[1,128,512]{2,1,0:T(8,128)(2,1)}, bf16[1,128,512]{2,1,0:T(8,128)(2,1)}, u32[]{:S(2)}, u32[]{:S(2)}) collective-permute-start(bf16[1,128,512]{2,1,0:T(8,128)(2,1)} %get-tuple-element.4), channel_id=1, source_target_pairs={{1,0},{2,1},{3,2},{4,3},{5,4},{6,5},{7,6},{8,7},{9,8},{10,9},{11,1... | collective-permute-start | bytes 393224 | tf_op jit(solution)/shard_map/ppermute | solution.py:18
  100.4 0.0 collective-permute-done.2
  100.4 4.5 %fusion.13 = f32[32,512,128]{1,2,0:T(8,128)} fusion(bf16[32,128,512]{2,1,0:T(8,128)(2,1)S(1)} %copy-done.4, bf16[1,128,512]{2,1,0:T(8,128)(2,1)S(1)} %collective-permute-done.2, bf16[32,3,128,128]{3,2,1,0:T(8,128)(2,1)S(1)} %copy-done.6), kind=kOutput, calls=%fused_computation.28 | convolution fusion | flops 545259520 | bytes 13762560 | tf_op jit(solution)/shard_map/itr,irc->itc/dot_general | solution.py:63
  104.8 0.0 all-to-all-done.2
  104.8 6.8 %fusion.7 = f32[32,128,512]{2,1,0:T(8,128)} fusion(bf16[512,512,1]{1,0,2:T(8,128)(2,1)} %bitcast.24, pred[32,512]{1,0:T(8,128)(4,1)S(1)} %copy-done.10, bf16[512,128]{0,1:T(8,128)(2,1)S(1)} %copy.29), kind=kOutput, calls=%fused_computation.20 | convolution fusion | flops 2149580800 | bytes 9060352 | tf_op jit(solution)/shard_map/tqr,qc->trc/dot_general | solution.py:66
  111.6 0.0 collective-permute-done.3
  111.6 13.7 %multiply_reduce_fusion = (f32[32,128]{1,0:T(8,128)S(1)}, f32[32,128,512]{2,1,0:T(8,128)}) fusion(f32[32,128]{1,0:T(8,128)S(1)} %scatter_fusion, f32[32,128,512]{2,1,0:T(8,128)} %fusion.7, bf16[1,128,512]{2,1,0:T(8,128)(2,1)} %collective-permute-done.3, bf16[32,128,512]{2,1,0:T(8,128)(2,1)S(1)} %copy-done.5, bf16[32,3,128,128]{3,2,1,0:T(8,128)(2,1)} %param.9, ...), kind=kOutput, calls=%fused_computation.17 | convolution fusion | flops 557838336 | bytes 38961152 | tf_op jit(solution)/shard_map/itr,irc->itc/dot_general | solution.py:63
  125.4 5.0 %fusion.3 = bf16[32,128,512]{2,1,0:T(8,128)(2,1)S(1)} fusion(f32[32,128,512]{2,1,0:T(8,128)} %get-tuple-element.11, f32[32,128]{1,0:T(8,128)S(1)} %maximum_multiply_fusion, pred[32,128]{1,0:T(8,128)(4,1)S(1)} %compare_bitcast_fusion, bf16[4096,512]{1,0:T(8,128)(2,1)S(1)} %copy-done.2), kind=kLoop, calls=%fused_computation.10 | loop fusion | flops 8388608 | bytes 16797696 | tf_op jit(solution)/shard_map/convert_element_type | solution.py:72
  130.4 0.0 copy-start.7
  130.4 3.1 %fusion.5 = (f32[32]{0:T(128)S(1)}, f32[32]{0:T(128)S(1)}) fusion(bf16[32,128,512]{2,1,0:T(8,128)(2,1)S(1)} %bitcast.81, bf16[32,128,512]{2,1,0:T(8,128)(2,1)S(1)} %copy-done.5, bf16[32,128,512]{2,1,0:T(8,128)(2,1)S(1)} %fusion.3), kind=kLoop, calls=%fused_computation.12 | loop fusion | flops 18874304 | bytes 12583168 | tf_op jit(solution)/shard_map/reduce_sum | solution.py:74
  133.4 0.6 pad_maximum_fusion.12
  (15 shorter events, 0.1 us)
Async XLA Ops:
  0.6 34.7 %copy-start.6 = (bf16[32,3,128,128]{3,2,1,0:T(8,128)(2,1)S(1)}, bf16[32,3,128,128]{3,2,1,0:T(8,128)(2,1)}, u32[]{:S(2)}) copy-start(bf16[32,3,128,128]{3,2,1,0:T(8,128)(2,1)} %param.9) | copy-start | bytes 9437188
  0.6 22.0 %copy-start.8 = (bf16[1,32,2,8,128]{4,3,2,1,0:T(8,128)(2,1)S(1)}, bf16[1,32,2,8,128]{4,3,2,1,0:T(8,128)(2,1)}, u32[]{:S(2)}) copy-start(bf16[1,32,2,8,128]{4,3,2,1,0:T(8,128)(2,1)} %param.13) | copy-start | bytes 393220
  2.2 22.7 %all-to-all-start = ((s32[1,32,2]{2,0,1:T(1,128)}), s32[1,32,2]{2,0,1:T(1,128)}, u32[]{:S(2)}, u32[]{:S(2)}) async-start(s32[1,32,2]{2,0,1:T(1,128)} %copy.30), calls=%async_computation | async-start | bytes 32768 | tf_op jit(solution)/shard_map/all_to_all | solution.py:40
  11.4 46.3 %collective-permute-start.1 = (bf16[1,128,512]{2,1,0:T(8,128)(2,1)}, bf16[1,128,512]{2,1,0:T(8,128)(2,1)}, u32[]{:S(2)}, u32[]{:S(2)}) collective-permute-start(bf16[1,128,512]{2,1,0:T(8,128)(2,1)} %get-tuple-element.6), channel_id=1, source_target_pairs={{1,0},{2,1},{3,2},{4,3},{5,4},{6,5},{7,6},{8,7},{9,8},{10,9},{11,1... | collective-permute-start | bytes 393224 | tf_op jit(solution)/shard_map/ppermute | solution.py:18
  16.5 25.7 %collective-permute-start = (bf16[1,128,512]{2,1,0:T(8,128)(2,1)}, bf16[1,128,512]{2,1,0:T(8,128)(2,1)}, u32[]{:S(2)}, u32[]{:S(2)}) collective-permute-start(bf16[1,128,512]{2,1,0:T(8,128)(2,1)} %get-tuple-element.7), channel_id=1, source_target_pairs={{0,1},{1,2},{2,3},{3,4},{4,5},{5,6},{6,7},{7,8},{8,9},{9,10},{10,1... | collective-permute-start | bytes 393224 | tf_op jit(solution)/shard_map/ppermute | solution.py:15
  23.6 27.3 %copy-start.9 = (pred[32,512]{1,0:T(8,128)(4,1)}, pred[32,512]{1,0:T(8,128)(4,1)S(1)}, u32[]{:S(2)}) copy-start(pred[32,512]{1,0:T(8,128)(4,1)S(1)} %copy.28) | copy-start | bytes 49156
  29.5 21.4 %all-to-all-start.1 = ((bf16[32,2,8,512]{3,2,1,0:T(8,128)(2,1)}), bf16[32,2,8,512]{3,2,1,0:T(8,128)(2,1)}, u32[]{:S(2)}, u32[]{:S(2)}) async-start(bf16[32,2,8,512]{3,2,1,0:T(8,128)(2,1)} %bitcast.85), calls=%async_computation.1 | async-start | bytes 1048576 | tf_op jit(solution)/shard_map/all_to_all | solution.py:25
  35.3 6.8 %copy-start.11 = (s32[4096]{0:T(1024)S(1)}, s32[4096]{0:T(1024)}, u32[]{:S(2)}) copy-start(s32[4096]{0:T(1024)} %param.8) | copy-start | bytes 49156
  35.4 6.8 %copy-start = (bf16[4096,512]{1,0:T(8,128)(2,1)S(1)}, bf16[4096,512]{1,0:T(8,128)(2,1)}, u32[]{:S(2)}) copy-start(bf16[4096,512]{1,0:T(8,128)(2,1)} %param.7) | copy-start | bytes 12582916
  50.9 6.8 %copy-start.1 = (bf16[4096,512]{1,0:T(8,128)(2,1)S(1)}, bf16[4096,512]{1,0:T(8,128)(2,1)}, u32[]{:S(2)}) copy-start(bf16[4096,512]{1,0:T(8,128)(2,1)} %param.7) | copy-start | bytes 12582916
  76.3 2.0 %copy-start.3 = (bf16[32,128,512]{2,1,0:T(8,128)(2,1)}, bf16[32,128,512]{2,1,0:T(8,128)(2,1)S(1)}, u32[]{:S(2)}) copy-start(bf16[32,128,512]{2,1,0:T(8,128)(2,1)S(1)} %fusion.2) | copy-start | bytes 12582916
  79.0 21.4 %collective-permute-start.2 = (bf16[1,128,512]{2,1,0:T(8,128)(2,1)}, bf16[1,128,512]{2,1,0:T(8,128)(2,1)S(1)}, u32[]{:S(2)}, u32[]{:S(2)}) collective-permute-start(bf16[1,128,512]{2,1,0:T(8,128)(2,1)} %get-tuple-element.5), channel_id=1, source_target_pairs={{0,1},{1,2},{2,3},{3,4},{4,5},{5,6},{6,7},{7,8},{8,9},{9,10},{10,1... | collective-permute-start | bytes 393224 | tf_op jit(solution)/shard_map/ppermute | solution.py:15
  82.6 22.3 %all-to-all-start.2 = ((bf16[32,2,8,512]{3,2,1,0:T(8,128)(2,1)}), bf16[32,2,8,512]{3,2,1,0:T(8,128)(2,1)}, u32[]{:S(2)}, u32[]{:S(2)}) async-start(bf16[32,2,8,512]{3,2,1,0:T(8,128)(2,1)} %bitcast.84), calls=%async_computation.2 | async-start | bytes 1048576 | tf_op jit(solution)/shard_map/all_to_all | solution.py:25
  88.4 11.9 %copy-start.4 = (bf16[32,128,512]{2,1,0:T(8,128)(2,1)S(1)}, bf16[32,128,512]{2,1,0:T(8,128)(2,1)}, u32[]{:S(2)}) copy-start(bf16[32,128,512]{2,1,0:T(8,128)(2,1)} %copy-done.3) | copy-start | bytes 12582916
  95.2 9.6 %copy-start.10 = (pred[32,512]{1,0:T(8,128)(4,1)S(1)}, pred[32,512]{1,0:T(8,128)(4,1)}, u32[]{:S(2)}) copy-start(pred[32,512]{1,0:T(8,128)(4,1)} %copy-done.9) | copy-start | bytes 49156
  95.2 16.4 %collective-permute-start.3 = (bf16[1,128,512]{2,1,0:T(8,128)(2,1)}, bf16[1,128,512]{2,1,0:T(8,128)(2,1)}, u32[]{:S(2)}, u32[]{:S(2)}) collective-permute-start(bf16[1,128,512]{2,1,0:T(8,128)(2,1)} %get-tuple-element.4), channel_id=1, source_target_pairs={{1,0},{2,1},{3,2},{4,3},{5,4},{6,5},{7,6},{8,7},{9,8},{10,9},{11,1... | collective-permute-start | bytes 393224 | tf_op jit(solution)/shard_map/ppermute | solution.py:18
  104.8 6.8 %copy-start.5 = (bf16[32,128,512]{2,1,0:T(8,128)(2,1)S(1)}, bf16[32,128,512]{2,1,0:T(8,128)(2,1)}, u32[]{:S(2)}) copy-start(bf16[32,128,512]{2,1,0:T(8,128)(2,1)} %copy-done.3) | copy-start | bytes 12582916
  111.6 13.8 %copy-start.2 = (bf16[4096,512]{1,0:T(8,128)(2,1)S(1)}, bf16[4096,512]{1,0:T(8,128)(2,1)}, u32[]{:S(2)}) copy-start(bf16[4096,512]{1,0:T(8,128)(2,1)} %param.7) | copy-start | bytes 12582916
  130.4 3.1 %copy-start.7 = (bf16[32,128,512]{2,1,0:T(8,128)(2,1)}, bf16[32,128,512]{2,1,0:T(8,128)(2,1)S(1)}, u32[]{:S(2)}) copy-start(bf16[32,128,512]{2,1,0:T(8,128)(2,1)S(1)} %fusion.3) | copy-start | bytes 12582916
where the time goes:
time: 135 us; the launch traced here: 134 us
  matrix products  64.3 us (48%)
  starting transfers between devices  29.4 us (22%)
  other arithmetic  20.4 us (15%)
  local copies, waits for them, and re-layouts  15.7 us (12%)
  waiting for transfers between devices  3.36 us (2%)
    dot_general x6, matrix products, body(): jnp.einsum('itr,irc->itc', band_w[:, offset + 1], source, preferred_eleme...  50.8 us
    dot_general x2, matrix products, body(): jnp.einsum('tqr,qc->trc', placed, received.reshape(-1, classes), preferre...  13.5 us
    all_to_all x2, starting transfers between devices, fetch_blocks(): lax.all_to_all(blocks, 'node', split_axis=0, concat_axis=0, tiled=True)  11.7 us
    ppermute x2, starting transfers between devices, with_halo(): lax.ppermute(lax.slice_in_dim(block, 0, width, axis=dim), axis, backward)  10.2 us
    convert_element_type x2, other arithmetic, body(): fresh = jnp.where(seeded, clamped, scaled).astype(jnp.bfloat16)  9.95 us
    all_to_all x1, starting transfers between devices, body(): lax.all_to_all(far_block, 'node', split_axis=1, concat_axis=0, tiled=True)  7.45 us
    gather x2, local copies, waits for them, and re-layouts, fetch_blocks(): blocks = current.reshape(-1, block_rows, classes)[requests]  7.15 us
    unnamed x26, local copies, waits for them, and re-layouts  4.35 us
  transfers between devices with their start and end apart: 7, of which 1 were waited for; matrix products, arithmetic and copies ran while one was open for 41% of the time, Pallas kernels for 0%

commit v1 on v0

--- a/solution.py
+++ b/solution.py
@@ -4,6 +4,12 @@
 from jax.sharding import PartitionSpec as P
 
 ITERS = 2
+
+
+def exchange_blocks(block, axis, split, join):
+    pieces = jnp.split(block, lax.axis_size(axis), axis=split)
+    arrived = lax.all_to_all(jnp.stack(pieces), axis, 0, 0)
+    return jnp.concatenate(arrived, axis=join)
 
 
 def with_halo(block, sides, width):
@@ -37,9 +43,7 @@
     peer_count = far_w.shape[1]
     slot_count = far_w.shape[2]
     block_rows = far_w.shape[3]
-    requests = lax.all_to_all(far_block, "node", split_axis=1, concat_axis=0, tiled=True).reshape(
-        peer_count, slot_count
-    )
+    requests = exchange_blocks(far_block, "node", 1, 0).reshape(peer_count, slot_count)
     live_slots = jnp.arange(slot_count)[None, :] < far_count[0][:, None]
     weights = jnp.where(live_slots[:, :, None, None], far_w[0], jnp.zeros((), jnp.bfloat16))
     flat_tiles = far_tile[0].reshape(-1)

time: 135 us -> 154 us (1.14)
  local copies, waits for them, and re-layouts: 15.7 us -> 35.1 us
    unnamed x26 -> x56, local copies, waits for them, and re-layouts: 4.35 us -> 19.7 us
    split x0 -> x2, local copies, waits for them, and re-layouts: none -> 3.46 us  [exchange_blocks(): pieces = jnp.split(block, lax.axis_size(axis), axis=split)]
  transfers between devices with their start and end apart: 7 -> 7, of which waited for: 1 -> 1; matrix products, arithmetic and copies ran while one was open for 41% -> 36% of each run, Pallas kernels for 0% -> 0%
where the time goes in v1:
time: 154 us; the launch traced here: 153 us
  matrix products  64.2 us (42%)
  local copies, waits for them, and re-layouts  35.1 us (23%)
  starting transfers between devices  29.4 us (19%)
  other arithmetic  20.4 us (13%)
  waiting for transfers between devices  3.38 us (2%)
    dot_general x6, matrix products, body(): jnp.einsum('itr,irc->itc', band_w[:, offset + 1], source, preferred_eleme...  50.7 us
    unnamed x56, local copies, waits for them, and re-layouts  19.7 us
    dot_general x2, matrix products, body(): jnp.einsum('tqr,qc->trc', placed, received.reshape(-1, classes), preferre...  13.5 us
    all_to_all x2, starting transfers between devices, fetch_blocks(): lax.all_to_all(blocks, 'node', split_axis=0, concat_axis=0, tiled=True)  11.7 us
    ppermute x2, starting transfers between devices, with_halo(): lax.ppermute(lax.slice_in_dim(block, 0, width, axis=dim), axis, backward)  10.2 us
    convert_element_type x2, other arithmetic, body(): fresh = jnp.where(seeded, clamped, scaled).astype(jnp.bfloat16)  9.95 us
    all_to_all x1, starting transfers between devices, exchange_blocks(): arrived = lax.all_to_all(jnp.stack(pieces), axis, 0, 0)  7.45 us
    gather x2, local copies, waits for them, and re-layouts, fetch_blocks(): blocks = current.reshape(-1, block_rows, classes)[requests]  7.15 us
  transfers between devices with their start and end apart: 7, of which 1 were waited for; matrix products, arithmetic and copies ran while one was open for 36% of the time, Pallas kernels for 0%

profile of v1, /device:TPU:0, one launch (start us, length us, event | category | flops | bytes accessed | tf_op | source)
XLA Modules:
  0.0 153.4 jit_solution(6529493488995585212)
XLA Ops:
  0.7 1.6 %slice_reduce_fusion.1 = (s32[2]{0:T(128)S(1)}, s32[2]{0:T(128)S(1)}, s32[2]{0:T(128)S(1)}, s32[2]{0:T(128)S(1)}, s32[2]{0:T(128)S(1)}, /*index=5*/s32[2]{0:T(12...) fusion(s32[1,32,2]{1,2,0:T(2,128)} %param.10), kind=kLoop, calls=%fused_computation.104 | loop fusion | bytes 208 | tf_op jit(solution)/shard_map/split | solution.py:10
  2.2 1.9 %slice_reduce_fusion = (s32[2]{0:T(128)S(1)}, s32[2]{0:T(128)S(1)}, s32[2]{0:T(128)S(1)}, s32[2]{0:T(128)S(1)}, s32[2]{0:T(128)S(1)}, /*index=5*/s32[2]{0:T(128)...) fusion(s32[1,32,2]{1,2,0:T(2,128)} %param.10), kind=kLoop, calls=%fused_computation.103 | loop fusion | bytes 304 | tf_op jit(solution)/shard_map/split | solution.py:10
  4.1 0.6 constant_dynamic-update-slice_fusion.31
  4.7 0.6 constant_dynamic-update-slice_fusion.30
  5.2 0.6 constant_dynamic-update-slice_fusion.29
  5.8 0.5 constant_dynamic-update-slice_fusion.28
  6.3 0.6 constant_dynamic-update-slice_fusion.27
  6.9 0.5 constant_dynamic-update-slice_fusion.26
  7.5 0.5 constant_dynamic-update-slice_fusion.25
  8.5 0.6 constant_dynamic-update-slice_fusion.23
  9.0 0.5 constant_dynamic-update-slice_fusion.22
  9.6 0.5 constant_dynamic-update-slice_fusion.21
  10.1 0.6 constant_dynamic-update-slice_fusion.20
  10.7 0.5 constant_dynamic-update-slice_fusion.19
  11.2 0.5 constant_dynamic-update-slice_fusion.18
  11.7 0.6 constant_dynamic-update-slice_fusion.17
  12.3 0.5 constant_dynamic-update-slice_fusion.16
  12.8 0.6 constant_dynamic-update-slice_fusion.15
  13.4 0.5 constant_dynamic-update-slice_fusion.14
  13.9 0.5 constant_dynamic-update-slice_fusion.13
  14.5 0.5 constant_dynamic-update-slice_fusion.12
  15.0 0.6 constant_dynamic-update-slice_fusion.11
  15.5 0.6 constant_dynamic-update-slice_fusion.10
  16.1 0.6 constant_dynamic-update-slice_fusion.9
  16.7 0.6 constant_dynamic-update-slice_fusion.8
  17.3 0.5 constant_dynamic-update-slice_fusion.7
  17.8 0.5 constant_dynamic-update-slice_fusion.6
  18.3 0.6 constant_dynamic-update-slice_fusion.5
  18.9 0.5 constant_dynamic-update-slice_fusion.4
  19.4 0.6 constant_dynamic-update-slice_fusion.3
  20.0 0.5 constant_dynamic-update-slice_fusion.2
  20.5 0.5 constant_dynamic-update-slice_fusion.1
  21.0 0.6 constant_dynamic-update-slice_fusion
  21.6 7.5 %all-to-all-start = ((s32[32,1,1,2]{3,2,1,0:T(1,128)}), s32[32,1,1,2]{3,2,1,0:T(1,128)}, u32[]{:S(2)}, u32[]{:S(2)}) async-start(s32[32,1,1,2]{3,2,1,0:T(1,128)} %constant_dynamic-update-slice_fusion), calls=%async_computation | async-start | bytes 32768 | tf_op jit(solution)/shard_map/all_to_all | solution.py:11
  29.1 1.7 %slice_bitcast_fusion = (bf16[1,128,512]{2,1,0:T(8,128)(2,1)}, bf16[1,128,512]{2,1,0:T(8,128)(2,1)}) fusion(bf16[4096,512]{1,0:T(8,128)(2,1)} %param.7), kind=kLoop, calls=%fused_computation.59 | loop fusion | bytes 524288 | tf_op jit(solution)/shard_map/slice | solution.py:24
  30.8 5.1 %collective-permute-start.1 = (bf16[1,128,512]{2,1,0:T(8,128)(2,1)}, bf16[1,128,512]{2,1,0:T(8,128)(2,1)}, u32[]{:S(2)}, u32[]{:S(2)}) collective-permute-start(bf16[1,128,512]{2,1,0:T(8,128)(2,1)} %get-tuple-element.38), channel_id=1, source_target_pairs={{1,0},{2,1},{3,2},{4,3},{5,4},{6,5},{7,6},{8,7},{9,8},{10,9},{11,1... | collective-permute-start | bytes 393224 | tf_op jit(solution)/shard_map/ppermute | solution.py:24
  35.9 0.8 copy.111
  36.9 0.7 iota_compare_fusion.1
  37.9 0.5 fusion.39
  38.5 2.5 %convert_reduce_fusion = f32[32,128]{1,0:T(8,128)S(1)} fusion(bf16[32,3,128,128]{3,2,1,0:T(8,128)(2,1)} %param.9), kind=kLoop, calls=%fused_computation.19 | loop fusion | flops 3141632 | bytes 3162112 | tf_op jit(solution)/shard_map/reduce_sum | solution.py:52
  41.1 1.0 bitcast_select_fusion.1
  42.1 0.8 convert_reduce_fusion.1
  43.2 1.1 scatter_fusion
  44.3 0.8 copy.114
  45.3 3.6 %gather_fusion = bf16[64,8,512]{2,1,0:T(8,128)(2,1)} fusion(bf16[512,8,512]{2,1,0:T(8,128)(2,1)} %bitcast.141, s32[1024]{0:T(1024)S(1)} %pad_clamp_fusion), kind=kCustom, calls=%fused_computation | custom fusion | bytes 1048832 | tf_op jit(solution)/shard_map/gather | solution.py:30
  48.9 5.8 %all-to-all-start.1 = ((bf16[32,2,8,512]{3,2,1,0:T(8,128)(2,1)}), bf16[32,2,8,512]{3,2,1,0:T(8,128)(2,1)}, u32[]{:S(2)}, u32[]{:S(2)}) async-start(bf16[32,2,8,512]{3,2,1,0:T(8,128)(2,1)} %bitcast.149), calls=%async_computation.1 | async-start | bytes 1048576 | tf_op jit(solution)/shard_map/all_to_all | solution.py:31
  54.8 6.8 %fusion.29 = f32[32,128,512]{2,1,0:T(8,128)} fusion(bf16[32,128,512]{2,1,0:T(8,128)(2,1)} %bitcast.142, bf16[32,3,128,128]{3,2,1,0:T(8,128)(2,1)S(1)} %copy-done.6), kind=kOutput, calls=%fused_computation.46 | convolution fusion | flops 536870912 | bytes 13631488 | tf_op jit(solution)/shard_map/itr,irc->itc/dot_general | solution.py:67
  61.6 5.4 %fusion.17 = f32[32,512,128]{1,2,0:T(8,128)} fusion(bf16[32,128,512]{2,1,0:T(8,128)(2,1)S(1)} %bitcast.143, bf16[1,128,512]{2,1,0:T(8,128)(2,1)} %collective-permute-done, bf16[32,3,128,128]{3,2,1,0:T(8,128)(2,1)S(1)} %copy-done.6), kind=kOutput, calls=%fused_computation.34 | convolution fusion | flops 545259520 | bytes 13762560 | tf_op jit(solution)/shard_map/itr,irc->itc/dot_general | solution.py:67
  67.0 3.4 %all-to-all-done.1 = bf16[32,2,8,512]{3,2,1,0:T(8,128)(2,1)} async-done(((bf16[32,2,8,512]{3,2,1,0:T(8,128)(2,1)}), bf16[32,2,8,512]{3,2,1,0:T(8,128)(2,1)}, u32[]{:S(2)}, u32[]{:S(2)}) %all-to-all-start.1) | async-done | bytes 524320 | tf_op jit(solution)/shard_map/all_to_all | solution.py:31
  70.4 6.8 %fusion.9 = f32[32,128,512]{2,1,0:T(8,128)} fusion(bf16[512,512,1]{1,0,2:T(8,128)(2,1)} %bitcast.16, pred[32,512]{1,0:T(8,128)(4,1)S(1)} %copy.112, bf16[512,128]{0,1:T(8,128)(2,1)S(1)} %copy.113), kind=kOutput, calls=%fused_computation.22 | convolution fusion | flops 2149580800 | bytes 9060352 | tf_op jit(solution)/shard_map/tqr,qc->trc/dot_general | solution.py:70
  77.1 13.6 %multiply_reduce_fusion.1 = (f32[32,128]{1,0:T(8,128)S(1)}, f32[32,128,512]{2,1,0:T(8,128)}) fusion(f32[32,128]{1,0:T(8,128)S(1)} %scatter_fusion, f32[32,128,512]{2,1,0:T(8,128)} %fusion.9, bf16[1,128,512]{2,1,0:T(8,128)(2,1)} %collective-permute-done.1, bf16[32,128,512]{2,1,0:T(8,128)(2,1)S(1)} %bitcast.144, bf16[32,3,128,128]{3,2,1,0:T(8,128)(2,1)S(1)} %copy-done.6, ...), kind=kOutput, calls=%fused_computation.18 | convolution fusion | flops 557838336 | bytes 38961152 | tf_op jit(solution)/shard_map/itr,irc->itc/dot_general | solution.py:67
  90.7 5.0 %fusion.2 = bf16[32,128,512]{2,1,0:T(8,128)(2,1)S(1)} fusion(f32[32,128,512]{2,1,0:T(8,128)} %get-tuple-element.41, f32[32,128]{1,0:T(8,128)S(1)} %maximum_multiply_fusion.1, pred[32,128]{1,0:T(8,128)(4,1)S(1)} %compare_bitcast_fusion, bf16[4096,512]{1,0:T(8,128)(2,1)S(1)} %copy-done.1), kind=kLoop, calls=%fused_computation.9 | loop fusion | flops 8388608 | bytes 16797696 | tf_op jit(solution)/shard_map/convert_element_type | solution.py:76
  95.7 2.0 %copy-done.3 = bf16[32,128,512]{2,1,0:T(8,128)(2,1)} copy-done((bf16[32,128,512]{2,1,0:T(8,128)(2,1)}, bf16[32,128,512]{2,1,0:T(8,128)(2,1)S(1)}, u32[]{:S(2)}) %copy-start.3) | copy-done | bytes 4194328
  97.7 0.7 fusion.46
  98.4 3.6 %gather_fusion.1 = bf16[64,8,512]{2,1,0:T(8,128)(2,1)} fusion(bf16[512,8,512]{2,1,0:T(8,128)(2,1)} %bitcast.146, s32[1024]{0:T(1024)S(1)} %pad_clamp_fusion), kind=kCustom, calls=%fused_computation.1 | custom fusion | bytes 1048832 | tf_op jit(solution)/shard_map/gather | solution.py:30
  102.0 5.8 %all-to-all-start.2 = ((bf16[32,2,8,512]{3,2,1,0:T(8,128)(2,1)}), bf16[32,2,8,512]{3,2,1,0:T(8,128)(2,1)}, u32[]{:S(2)}, u32[]{:S(2)}) async-start(bf16[32,2,8,512]{3,2,1,0:T(8,128)(2,1)} %bitcast.148), calls=%async_computation.2 | async-start | bytes 1048576 | tf_op jit(solution)/shard_map/all_to_all | solution.py:31
  107.9 6.8 %fusion.27 = f32[32,512,128]{1,2,0:T(8,128)} fusion(bf16[32,128,512]{2,1,0:T(8,128)(2,1)} %copy-done.3, bf16[32,3,128,128]{3,2,1,0:T(8,128)(2,1)S(1)} %copy-done.6), kind=kOutput, calls=%fused_computation.44 | convolution fusion | flops 536870912 | bytes 13631488 | tf_op jit(solution)/shard_map/itr,irc->itc/dot_general | solution.py:67
  114.7 5.1 %collective-permute-start.3 = (bf16[1,128,512]{2,1,0:T(8,128)(2,1)}, bf16[1,128,512]{2,1,0:T(8,128)(2,1)}, u32[]{:S(2)}, u32[]{:S(2)}) collective-permute-start(bf16[1,128,512]{2,1,0:T(8,128)(2,1)} %get-tuple-element.36), channel_id=1, source_target_pairs={{1,0},{2,1},{3,2},{4,3},{5,4},{6,5},{7,6},{8,7},{9,8},{10,9},{11,1... | collective-permute-start | bytes 393224 | tf_op jit(solution)/shard_map/ppermute | solution.py:24
  119.8 4.5 %fusion.13 = f32[32,512,128]{1,2,0:T(8,128)} fusion(bf16[32,128,512]{2,1,0:T(8,128)(2,1)S(1)} %copy-done.4, bf16[1,128,512]{2,1,0:T(8,128)(2,1)S(1)} %collective-permute-done.2, bf16[32,3,128,128]{3,2,1,0:T(8,128)(2,1)S(1)} %copy-done.6), kind=kOutput, calls=%fused_computation.28 | convolution fusion | flops 545259520 | bytes 13762560 | tf_op jit(solution)/shard_map/itr,irc->itc/dot_general | solution.py:67
  124.3 6.8 %fusion.7 = f32[32,128,512]{2,1,0:T(8,128)} fusion(bf16[512,512,1]{1,0,2:T(8,128)(2,1)} %bitcast.24, pred[32,512]{1,0:T(8,128)(4,1)S(1)} %copy-done.10, bf16[512,128]{0,1:T(8,128)(2,1)S(1)} %copy.113), kind=kOutput, calls=%fused_computation.20 | convolution fusion | flops 2149580800 | bytes 9060352 | tf_op jit(solution)/shard_map/tqr,qc->trc/dot_general | solution.py:70
  131.0 13.7 %multiply_reduce_fusion = (f32[32,128]{1,0:T(8,128)S(1)}, f32[32,128,512]{2,1,0:T(8,128)}) fusion(f32[32,128]{1,0:T(8,128)S(1)} %scatter_fusion, f32[32,128,512]{2,1,0:T(8,128)} %fusion.7, bf16[1,128,512]{2,1,0:T(8,128)(2,1)} %collective-permute-done.3, bf16[32,128,512]{2,1,0:T(8,128)(2,1)S(1)} %copy-done.5, bf16[32,3,128,128]{3,2,1,0:T(8,128)(2,1)} %param.9, ...), kind=kOutput, calls=%fused_computation.17 | convolution fusion | flops 557838336 | bytes 38961152 | tf_op jit(solution)/shard_map/itr,irc->itc/dot_general | solution.py:67
  144.8 5.0 %fusion.3 = bf16[32,128,512]{2,1,0:T(8,128)(2,1)S(1)} fusion(f32[32,128,512]{2,1,0:T(8,128)} %get-tuple-element.43, f32[32,128]{1,0:T(8,128)S(1)} %maximum_multiply_fusion, pred[32,128]{1,0:T(8,128)(4,1)S(1)} %compare_bitcast_fusion, bf16[4096,512]{1,0:T(8,128)(2,1)S(1)} %copy-done.2), kind=kLoop, calls=%fused_computation.10 | loop fusion | flops 8388608 | bytes 16797696 | tf_op jit(solution)/shard_map/convert_element_type | solution.py:76
  149.8 3.1 %fusion.5 = (f32[32]{0:T(128)S(1)}, f32[32]{0:T(128)S(1)}) fusion(bf16[32,128,512]{2,1,0:T(8,128)(2,1)S(1)} %bitcast.145, bf16[32,128,512]{2,1,0:T(8,128)(2,1)S(1)} %copy-done.5, bf16[32,128,512]{2,1,0:T(8,128)(2,1)S(1)} %fusion.3), kind=kLoop, calls=%fused_computation.12 | loop fusion | flops 18874304 | bytes 12583168 | tf_op jit(solution)/shard_map/reduce_sum | solution.py:78
  152.8 0.6 pad_maximum_fusion.12
  (48 shorter events, 1.7 us)
Async XLA Ops:
  0.6 54.1 %copy-start.6 = (bf16[32,3,128,128]{3,2,1,0:T(8,128)(2,1)S(1)}, bf16[32,3,128,128]{3,2,1,0:T(8,128)(2,1)}, u32[]{:S(2)}) copy-start(bf16[32,3,128,128]{3,2,1,0:T(8,128)(2,1)} %param.9) | copy-start | bytes 9437188
  0.6 41.5 %copy-start.8 = (bf16[1,32,2,8,128]{4,3,2,1,0:T(8,128)(2,1)S(1)}, bf16[1,32,2,8,128]{4,3,2,1,0:T(8,128)(2,1)}, u32[]{:S(2)}) copy-start(bf16[1,32,2,8,128]{4,3,2,1,0:T(8,128)(2,1)} %param.13) | copy-start | bytes 393220
  21.6 22.7 %all-to-all-start = ((s32[32,1,1,2]{3,2,1,0:T(1,128)}), s32[32,1,1,2]{3,2,1,0:T(1,128)}, u32[]{:S(2)}, u32[]{:S(2)}) async-start(s32[32,1,1,2]{3,2,1,0:T(1,128)} %constant_dynamic-update-slice_fusion), calls=%async_computation | async-start | bytes 32768 | tf_op jit(solution)/shard_map/all_to_all | solution.py:11
  30.8 46.3 %collective-permute-start.1 = (bf16[1,128,512]{2,1,0:T(8,128)(2,1)}, bf16[1,128,512]{2,1,0:T(8,128)(2,1)}, u32[]{:S(2)}, u32[]{:S(2)}) collective-permute-start(bf16[1,128,512]{2,1,0:T(8,128)(2,1)} %get-tuple-element.38), channel_id=1, source_target_pairs={{1,0},{2,1},{3,2},{4,3},{5,4},{6,5},{7,6},{8,7},{9,8},{10,9},{11,1... | collective-permute-start | bytes 393224 | tf_op jit(solution)/shard_map/ppermute | solution.py:24
  35.9 25.7 %collective-permute-start = (bf16[1,128,512]{2,1,0:T(8,128)(2,1)}, bf16[1,128,512]{2,1,0:T(8,128)(2,1)}, u32[]{:S(2)}, u32[]{:S(2)}) collective-permute-start(bf16[1,128,512]{2,1,0:T(8,128)(2,1)} %get-tuple-element.39), channel_id=1, source_target_pairs={{0,1},{1,2},{2,3},{3,4},{4,5},{5,6},{6,7},{7,8},{8,9},{9,10},{10,1... | collective-permute-start | bytes 393224 | tf_op jit(solution)/shard_map/ppermute | solution.py:21
  43.0 27.3 %copy-start.9 = (pred[32,512]{1,0:T(8,128)(4,1)}, pred[32,512]{1,0:T(8,128)(4,1)S(1)}, u32[]{:S(2)}) copy-start(pred[32,512]{1,0:T(8,128)(4,1)S(1)} %copy.112) | copy-start | bytes 49156
  48.9 21.4 %all-to-all-start.1 = ((bf16[32,2,8,512]{3,2,1,0:T(8,128)(2,1)}), bf16[32,2,8,512]{3,2,1,0:T(8,128)(2,1)}, u32[]{:S(2)}, u32[]{:S(2)}) async-start(bf16[32,2,8,512]{3,2,1,0:T(8,128)(2,1)} %bitcast.149), calls=%async_computation.1 | async-start | bytes 1048576 | tf_op jit(solution)/shard_map/all_to_all | solution.py:31
  54.8 6.8 %copy-start.11 = (s32[4096]{0:T(1024)S(1)}, s32[4096]{0:T(1024)}, u32[]{:S(2)}) copy-start(s32[4096]{0:T(1024)} %param.8) | copy-start | bytes 49156
  54.8 6.8 %copy-start = (bf16[4096,512]{1,0:T(8,128)(2,1)S(1)}, bf16[4096,512]{1,0:T(8,128)(2,1)}, u32[]{:S(2)}) copy-start(bf16[4096,512]{1,0:T(8,128)(2,1)} %param.7) | copy-start | bytes 12582916
  70.4 6.8 %copy-start.1 = (bf16[4096,512]{1,0:T(8,128)(2,1)S(1)}, bf16[4096,512]{1,0:T(8,128)(2,1)}, u32[]{:S(2)}) copy-start(bf16[4096,512]{1,0:T(8,128)(2,1)} %param.7) | copy-start | bytes 12582916
  95.7 2.0 %copy-start.3 = (bf16[32,128,512]{2,1,0:T(8,128)(2,1)}, bf16[32,128,512]{2,1,0:T(8,128)(2,1)S(1)}, u32[]{:S(2)}) copy-start(bf16[32,128,512]{2,1,0:T(8,128)(2,1)S(1)} %fusion.2) | copy-start | bytes 12582916
  98.4 21.4 %collective-permute-start.2 = (bf16[1,128,512]{2,1,0:T(8,128)(2,1)}, bf16[1,128,512]{2,1,0:T(8,128)(2,1)S(1)}, u32[]{:S(2)}, u32[]{:S(2)}) collective-permute-start(bf16[1,128,512]{2,1,0:T(8,128)(2,1)} %get-tuple-element.37), channel_id=1, source_target_pairs={{0,1},{1,2},{2,3},{3,4},{4,5},{5,6},{6,7},{7,8},{8,9},{9,10},{10,1... | collective-permute-start | bytes 393224 | tf_op jit(solution)/shard_map/ppermute | solution.py:21
  102.0 22.2 %all-to-all-start.2 = ((bf16[32,2,8,512]{3,2,1,0:T(8,128)(2,1)}), bf16[32,2,8,512]{3,2,1,0:T(8,128)(2,1)}, u32[]{:S(2)}, u32[]{:S(2)}) async-start(bf16[32,2,8,512]{3,2,1,0:T(8,128)(2,1)} %bitcast.148), calls=%async_computation.2 | async-start | bytes 1048576 | tf_op jit(solution)/shard_map/all_to_all | solution.py:31
  107.8 11.9 %copy-start.4 = (bf16[32,128,512]{2,1,0:T(8,128)(2,1)S(1)}, bf16[32,128,512]{2,1,0:T(8,128)(2,1)}, u32[]{:S(2)}) copy-start(bf16[32,128,512]{2,1,0:T(8,128)(2,1)} %copy-done.3) | copy-start | bytes 12582916
  114.7 9.6 %copy-start.10 = (pred[32,512]{1,0:T(8,128)(4,1)S(1)}, pred[32,512]{1,0:T(8,128)(4,1)}, u32[]{:S(2)}) copy-start(pred[32,512]{1,0:T(8,128)(4,1)} %copy-done.9) | copy-start | bytes 49156
  114.7 16.4 %collective-permute-start.3 = (bf16[1,128,512]{2,1,0:T(8,128)(2,1)}, bf16[1,128,512]{2,1,0:T(8,128)(2,1)}, u32[]{:S(2)}, u32[]{:S(2)}) collective-permute-start(bf16[1,128,512]{2,1,0:T(8,128)(2,1)} %get-tuple-element.36), channel_id=1, source_target_pairs={{1,0},{2,1},{3,2},{4,3},{5,4},{6,5},{7,6},{8,7},{9,8},{10,9},{11,1... | collective-permute-start | bytes 393224 | tf_op jit(solution)/shard_map/ppermute | solution.py:24
  124.3 6.8 %copy-start.5 = (bf16[32,128,512]{2,1,0:T(8,128)(2,1)S(1)}, bf16[32,128,512]{2,1,0:T(8,128)(2,1)}, u32[]{:S(2)}) copy-start(bf16[32,128,512]{2,1,0:T(8,128)(2,1)} %copy-done.3) | copy-start | bytes 12582916
  131.0 13.7 %copy-start.2 = (bf16[4096,512]{1,0:T(8,128)(2,1)S(1)}, bf16[4096,512]{1,0:T(8,128)(2,1)}, u32[]{:S(2)}) copy-start(bf16[4096,512]{1,0:T(8,128)(2,1)} %param.7) | copy-start | bytes 12582916
  149.7 3.1 %copy-start.7 = (bf16[32,128,512]{2,1,0:T(8,128)(2,1)}, bf16[32,128,512]{2,1,0:T(8,128)(2,1)S(1)}, u32[]{:S(2)}) copy-start(bf16[32,128,512]{2,1,0:T(8,128)(2,1)S(1)} %fusion.3) | copy-start | bytes 12582916
